TPU v7x, 32 devices: a whole 2x2x4 slice. The times are simulated.
32 devices in a mesh: parts: 2 (over x), cluster: 16 (over z, y, core).
Axes of the slice: x: 2, y: 2, z: 4, core: 2. Of those that a mesh axis runs over, the one named last changes fastest.
Arguments:
- queries: float32 [4096, 1024], P(('parts', 'cluster')), parts along dimension 0, may hold values from -1 to 1
- passages: float32 [64, 128, 1024], P(('parts', 'cluster')), parts along dimension 0, may hold values from -6 to 6
- first_blocks: int32 [4096, 4], P(('parts', 'cluster')), parts along dimension 0, may hold values from 0 to 31, all different within a row; in each aligned block of 128 rows (0 to 127, 128 to 255, ...) at most 24 rows name the same one
- followup_blocks: int32 [4096, 4], P(('parts', 'cluster')), parts along dimension 0, may hold values from 0 to 31, all different within a row; in each aligned block of 128 rows (0 to 127, 128 to 255, ...) at most 24 rows name the same one
Outputs:
- expanded: float32 [4096, 1024], P(('parts', 'cluster')), parts along dimension 0
- second_scores: float32 [4096, 4, 128], P(('parts', 'cluster')), parts along dimension 0
There are 2 independent parts, one for each index of `parts`. A program takes and returns all parts, laid end to end along the dimension named above; each array names one. Nothing has to cross between parts.
Inputs may be any that keep to these rules, and one draw needn't show every extreme that they name: `first_blocks`: each row names 4 different blocks; among the queries of one device no block is named more than 24 times, and some block is named exactly 24 times. `followup_blocks`: each row names 4 different blocks; among the queries of one device no block is named more than 24 times, and some block is named exactly 24 times.
All inputs are finite; a program needn't handle non-finite values.
Results may differ from a plain program's by a relative error of at most 0.00014.
Values sent between devices are 32-bit elements; how exact they have to be, the bound alone decides.
A program may use at most 128 MiB of HBM per device.

v0:
```python
import functools

import jax
import jax.numpy as jnp
from jax import lax
from jax.experimental import pallas as pl
from jax.experimental.pallas import tpu as pltpu
from jax.sharding import PartitionSpec as P

SOFTMAX_HEAT = 2.0
FEEDBACK = 0.5
MASKED = -1e30
VMEM_BYTES = 63 * 1024 * 1024


def position_targets(block_ids, capacity):
    flat_ids = block_ids.reshape(-1)
    matches = flat_ids[:, None] == flat_ids[None, :]
    positions = jnp.arange(flat_ids.shape[0], dtype=jnp.int32)
    earlier = positions[None, :] < positions[:, None]
    ranking = jnp.sum(jnp.logical_and(matches, earlier), axis=1, dtype=jnp.int32)
    return flat_ids * capacity + ranking


def pack_rows(values, targets, owners, resident_blocks, capacity):
    buffer = jnp.zeros((owners * resident_blocks * capacity, values.shape[1]), values.dtype)
    buffer = buffer.at[targets].set(values)
    return buffer.reshape(owners, resident_blocks, capacity, values.shape[1])


def reply(results):
    return (
        lax.all_to_all(results[0], "cluster", split_axis=0, concat_axis=0, tiled=True),
        lax.all_to_all(results[1], "cluster", split_axis=0, concat_axis=0, tiled=True),
        lax.all_to_all(results[2], "cluster", split_axis=0, concat_axis=0, tiled=True),
    )


def send_back(match_scores):
    return lax.all_to_all(match_scores, "cluster", split_axis=0, concat_axis=0, tiled=True)


def local(queries, passages, first_blocks, followup_blocks):
    owners = lax.axis_size("cluster")
    resident_blocks = passages.shape[0]
    embed_width = queries.shape[1]
    per_query = first_blocks.shape[1]
    pair_count = queries.shape[0] * per_query
    all_blocks = owners * resident_blocks
    capacity = max(2, (3 * pair_count + 2 * all_blocks - 1) // (2 * all_blocks))
    coefficient = FEEDBACK * embed_width ** (-0.5)
    highest = lax.Precision.HIGHEST

    def project_onto_centroid(arrived):
        return jnp.einsum("nbce,bre->nbcr", arrived, passages, precision=highest)

    first_targets = position_targets(first_blocks, capacity)
    second_targets = position_targets(followup_blocks, capacity)
    repeated = jnp.repeat(queries, per_query, axis=0)
    first_sent = pack_rows(repeated, first_targets, owners, resident_blocks, capacity)
    match_scores = SOFTMAX_HEAT * project_onto_centroid(
        lax.all_to_all(first_sent, "cluster", split_axis=0, concat_axis=0, tiled=True)
    )
    highs = jnp.max(match_scores, axis=3)
    weights = jnp.exp(match_scores - highs[..., None])
    totals = jnp.sum(weights, axis=3)
    vectors = jnp.einsum("nbcr,bre->nbce", weights, passages, precision=highest)
    highs, totals, vectors = reply((highs, totals, vectors))
    highs = highs.reshape(-1)[first_targets].reshape(-1, per_query)
    totals = totals.reshape(-1)[first_targets].reshape(-1, per_query)
    vectors = vectors.reshape(-1, embed_width)[first_targets].reshape(-1, per_query, embed_width)
    peak_high = jnp.max(highs, axis=1, keepdims=True)
    scaled = jnp.exp(highs - peak_high)
    denominator = jnp.sum(scaled * totals, axis=1)
    feedback = jnp.einsum("qk,qke->qe", scaled, vectors, precision=highest) / denominator[:, None]
    expanded = queries + coefficient * feedback
    expanded_sent = pack_rows(
        jnp.repeat(expanded, per_query, axis=0), second_targets, owners, resident_blocks, capacity
    )
    returned = (lambda arrived: send_back(project_onto_centroid(arrived)))(
        lax.all_to_all(expanded_sent, "cluster", split_axis=0, concat_axis=0, tiled=True)
    )
    second_scores = returned.reshape(-1, returned.shape[3])[second_targets].reshape(
        queries.shape[0], per_query, -1
    )
    return (expanded, second_scores)


def dot_nt(a, b):
    return lax.dot_general(a, b, (((1,), (1,)), ((), ())), preferred_element_type=jnp.float32)


def dot_nn(a, b):
    return lax.dot_general(a, b, (((1,), (0,)), ((), ())), preferred_element_type=jnp.float32)


def halves(x):
    high = x.astype(jnp.bfloat16)
    return high, (x - high.astype(jnp.float32)).astype(jnp.bfloat16)


def ring_kernel(
    chips, queries_in, passages, first, followup, expanded, scores,
    corpus, corpus_hi, corpus_lo, queries, pair, total, asked, chosen, picked,
    load_sem, send_r, recv_r, send_l, recv_l, send_a, recv_a, send_b, recv_b,
):
    me = lax.axis_index("cluster")
    chip, core = me // 2, me % 2
    rows, width = queries.shape
    top = first.shape[0]
    size = passages.shape[1]
    half = chips // 2
    spot = (1 - chip % 2) * (chip // 2) + (chip % 2) * (chips - 1 - chip // 2)

    def chip_at(position):
        position = (position + chips) % chips
        late = position // half
        return (1 - late) * (2 * position) + late * (2 * (chips - 1 - position) + 1)

    right = 2 * chip_at(spot + 1) + core
    left = 2 * chip_at(spot + chips - 1) + core
    other = 2 * chip + 1 - core

    def remote(src, dst, send, recv, device):
        return pltpu.make_async_remote_copy(
            src_ref=src, dst_ref=dst, send_sem=send, recv_sem=recv,
            device_id={"cluster": device}, device_id_type=pl.DeviceIdType.MESH,
        )

    def rightward(step, src):
        return remote(src, corpus.at[step, 0], send_r.at[step], recv_r.at[step], right)

    def leftward(step, src):
        return remote(src, corpus.at[step, 1], send_l.at[step], recv_l.at[step], left)

    def across_a(step):
        return remote(corpus.at[step, 0], corpus.at[step, 2], send_a.at[step], recv_a.at[step], other)

    def across_b(step):
        return remote(corpus.at[step, 1], corpus.at[step, 3], send_b.at[step], recv_b.at[step], other)

    def blocks_of(step):
        away = (step + 1) // 2
        from_left = 2 * chip_at(spot + chips - away)
        from_right = 2 * chip_at(spot + away)
        a, b = (step + 1) % 2, step % 2
        return (
            (from_left + core) * 2 + a,
            (from_right + core) * 2 + b,
            (from_left + 1 - core) * 2 + a,
            (from_right + 1 - core) * 2 + b,
        )

    loads = (
        pltpu.make_async_copy(passages.at[1], corpus.at[0, 0], load_sem.at[0]),
        pltpu.make_async_copy(passages.at[0], corpus.at[0, 1], load_sem.at[1]),
        pltpu.make_async_copy(queries_in, queries, load_sem.at[2]),
    )
    for load in loads:
        load.start()
    barrier = pltpu.get_barrier_semaphore()
    for device in (right, left, other):
        pl.semaphore_signal(
            barrier, inc=1, device_id={"cluster": device}, device_id_type=pl.DeviceIdType.MESH
        )
    pl.semaphore_wait(barrier, 3)
    for load in loads[:2]:
        load.wait()
    rightward(1, corpus.at[0, 1]).start()
    leftward(1, corpus.at[0, 0]).start()
    for load in loads[2:]:
        load.wait()

    def put_pair(x):
        high, low = halves(x)
        pair[pl.ds(0, rows), :] = high
        pair[pl.ds(rows, rows), :] = low

    put_pair(queries[...])
    total[...] = jnp.zeros_like(total)
    for j in range(top):
        asked[j] = jnp.broadcast_to(first[j : j + 1, :].astype(jnp.float32), (size, rows)).T
        chosen[j] = jnp.broadcast_to(followup[j : j + 1, :].astype(jnp.float32), (size, rows))
    picked[...] = jnp.zeros_like(picked)

    def absorb(step, slot, carry):
        peak, norm = carry
        place = pl.ds(slot * size, 2 * size)
        for t in (slot, slot + 1):
            high, low = halves(corpus[step, t])
            corpus_hi[step, pl.ds(t * size, size), :] = high
            corpus_lo[step, pl.ds(t * size, size), :] = low
        both = dot_nt(pair[...], corpus_hi[step, place, :])
        found = SOFTMAX_HEAT * (
            both[:rows] + both[rows:] + dot_nt(pair[pl.ds(0, rows), :], corpus_lo[step, place, :])
        )
        parts, hits = [], []
        top_score = peak
        for t, block in enumerate(blocks_of(step)[slot : slot + 2]):
            name = block.astype(jnp.float32)
            hit = asked[0] == name
            for j in range(1, top):
                hit = jnp.logical_or(hit, asked[j] == name)
            part = jnp.where(hit, found[:, t * size : (t + 1) * size], MASKED)
            top_score = jnp.maximum(top_score, jnp.max(part, axis=1, keepdims=True))
            parts.append(part)
            hits.append(hit)
        shrink = jnp.exp(peak - top_score)
        weights = jnp.concatenate(
            [jnp.where(hit, jnp.exp(part - top_score), 0.0) for hit, part in zip(hits, parts)], axis=1
        )
        norm = norm * shrink + jnp.sum(weights, axis=1, keepdims=True)
        high, low = halves(weights)
        mixed = dot_nn(jnp.concatenate([high, low], axis=0), corpus_hi[step, place, :])
        total[...] = total[...] * shrink + (
            mixed[:rows] + mixed[rows:] + dot_nn(high, corpus_lo[step, place, :])
        )
        return top_score, norm

    def first_round(step, carry):
        @pl.when(step > 0)
        def _():
            rightward(step, corpus.at[step, 0]).wait_recv()
            leftward(step, corpus.at[step, 1]).wait_recv()

        @pl.when(step < chips - 2)
        def _():
            rightward(step + 2, corpus.at[step, 0]).start()
            leftward(step + 2, corpus.at[step, 1]).start()

        across_a(step).start()
        across_b(step).start()
        carry = absorb(step, 0, carry)
        across_a(step).wait_recv()
        across_b(step).wait_recv()
        return absorb(step, 2, carry)

    start = (jnp.full((rows, 1), MASKED, jnp.float32), jnp.zeros((rows, 1), jnp.float32))
    _, norm = lax.fori_loop(0, chips, first_round, start)

    after = queries[...] + (FEEDBACK * width ** (-0.5)) * (total[...] / norm)
    expanded[...] = after
    put_pair(after)

    def second_round(step, carry):
        both = dot_nt(corpus_hi[step], pair[...])
        found = both[:, :rows] + both[:, rows:] + dot_nt(corpus_lo[step], pair[pl.ds(0, rows), :])
        ids = [block.astype(jnp.float32) for block in blocks_of(step)]
        for j in range(top):
            names = chosen[j]
            value = picked[j]
            for t in range(4):
                value = jnp.where(names == ids[t], found[t * size : (t + 1) * size, :], value)
            picked[j] = value
        return carry

    lax.fori_loop(0, chips, second_round, 0)
    for j in range(top):
        scores[:, j, :] = picked[j].T

    def drain(step, carry):
        @pl.when(step > 0)
        def _():
            rightward(step, corpus.at[step, 0]).wait_send()
            leftward(step, corpus.at[step, 1]).wait_send()

        across_a(step).wait_send()
        across_b(step).wait_send()
        return carry

    lax.fori_loop(0, chips, drain, 0)


def grant_of(queries, passages, first_blocks):
    resident, size, width = passages.shape
    rows = queries.shape[0]
    corpus = lax.axis_size("cluster") * resident * size * width * 8
    return corpus + (10 * rows * width + 6 * first_blocks.shape[1] * rows * size) * 4


def ring_fits(queries, passages, first_blocks):
    owners = lax.axis_size("cluster")
    resident, size, _ = passages.shape
    fits = grant_of(queries, passages, first_blocks) < VMEM_BYTES
    return owners % 4 == 0 and resident == 2 and fits and queries.shape[0] == size


def device_program(queries, passages, first_blocks, followup_blocks):
    if not ring_fits(queries, passages, first_blocks):
        return local(queries, passages, first_blocks, followup_blocks)
    chips = lax.axis_size("cluster") // 2
    rows, width = queries.shape
    size = passages.shape[1]
    top = first_blocks.shape[1]
    vmem = pl.BlockSpec(memory_space=pltpu.VMEM)
    hbm = pl.BlockSpec(memory_space=pltpu.HBM)
    return pl.pallas_call(
        functools.partial(ring_kernel, chips),
        out_shape=(
            jax.ShapeDtypeStruct((rows, width), jnp.float32),
            jax.ShapeDtypeStruct((rows, top, size), jnp.float32),
        ),
        in_specs=[hbm, hbm, vmem, vmem],
        out_specs=(vmem, vmem),
        scratch_shapes=[
            pltpu.VMEM((chips, 4, size, width), jnp.float32),
            pltpu.VMEM((chips, 4 * size, width), jnp.bfloat16),
            pltpu.VMEM((chips, 4 * size, width), jnp.bfloat16),
            pltpu.VMEM((rows, width), jnp.float32),
            pltpu.VMEM((2 * rows, width), jnp.bfloat16),
            pltpu.VMEM((rows, width), jnp.float32),
            pltpu.VMEM((top, rows, size), jnp.float32),
            pltpu.VMEM((top, size, rows), jnp.float32),
            pltpu.VMEM((top, size, rows), jnp.float32),
            pltpu.SemaphoreType.DMA((3,)),
        ]
        + [pltpu.SemaphoreType.DMA((chips,))] * 8,
        compiler_params=pltpu.CompilerParams(
            collective_id=0, has_side_effects=True, vmem_limit_bytes=VMEM_BYTES
        ),
    )(queries, passages, first_blocks.T, followup_blocks.T)


def solution(mesh):
    return jax.shard_map(
        device_program,
        mesh=mesh,
        in_specs=(
            P(("parts", "cluster"), None),
            P(("parts", "cluster"), None, None),
            P(("parts", "cluster"), None),
            P(("parts", "cluster"), None),
        ),
        out_specs=(P(("parts", "cluster"), None), P(("parts", "cluster"), None, None)),
        check_vma=False,
    )
```

profile of v0, /device:TPU:1, one launch (start us, length us, event | category | flops | bytes accessed | tf_op | source)
XLA Modules:
  0.0 99.1 jit_solution(11742507859194288515)
XLA Ops:
  0.6 95.8 %shard_map.59 = (f32[128,1024]{1,0:T(8,128)}, f32[128,4,128]{2,1,0:T(4,128)}) custom-call(f32[128,1024]{1,0:T(8,128)} %queries_in.1, f32[2,128,1024]{2,1,0:T(8,128)} %passages.1, s32[4,128]{1,0:T(4,128)} %bitcast.2, s32[4,128]{1,0:T(4,128)} %bitcast.3), custom_call_target="tpu_custom_call" | custom-call | tf_op jit(solution)/shard_map/pallas_call | solution.py:297
  96.4 0.0 copy-start
  96.5 1.9 %copy.8 = f32[128,1024]{1,0:T(8,128)} copy(f32[128,1024]{1,0:T(8,128)} %get-tuple-element.4) | data formatting | bytes 1048576
  98.4 0.0 copy-done
  98.4 0.7 copy.9
Async XLA Ops:
  96.4 1.9 %copy-start = (f32[128,4,128]{2,1,0:T(4,128)S(1)}, f32[128,4,128]{2,1,0:T(4,128)}, u32[]{:S(2)}) copy-start(f32[128,4,128]{2,1,0:T(4,128)} %get-tuple-element.5) | copy-start | bytes 786436
where the time goes:
time: 99.3 us; the launch traced here: 99.1 us
  Pallas kernels  95.8 us (96%)
  local copies, waits for them, and re-layouts  2.63 us (3%)
    pallas_call x1, Pallas kernels, device_program(): pl.pallas_call(functools.partial(ring_kernel, chips), out_shape=(jax.Shap...  95.8 us
    unnamed x4, local copies, waits for them, and re-layouts  2.63 us

commit v1 on v0

--- a/solution.py
+++ b/solution.py
@@ -10,7 +10,7 @@
 SOFTMAX_HEAT = 2.0
 FEEDBACK = 0.5
 MASKED = -1e30
-VMEM_BYTES = 63 * 1024 * 1024
+VMEM_BYTES = 50 * 1024 * 1024
 
 
 def position_targets(block_ids, capacity):
@@ -100,8 +100,8 @@
 
 
 def ring_kernel(
-    chips, queries_in, passages, first, followup, expanded, scores,
-    corpus, corpus_hi, corpus_lo, queries, pair, total, asked, chosen, picked,
+    chips, queries_in, passages, first_in, followup_in, expanded, scores,
+    first, followup, corpus, turned_hi, turned_lo, queries, pair, total, asked, chosen, picked,
     load_sem, send_r, recv_r, send_l, recv_l, send_a, recv_a, send_b, recv_b,
 ):
     me = lax.axis_index("cluster")
@@ -109,7 +109,9 @@
     rows, width = queries.shape
     top = first.shape[0]
     size = passages.shape[1]
+    piece = size // 2
     half = chips // 2
+    last = chips - 1
     spot = (1 - chip % 2) * (chip // 2) + (chip % 2) * (chips - 1 - chip // 2)
 
     def chip_at(position):
@@ -138,6 +140,32 @@
 
     def across_b(step):
         return remote(corpus.at[step, 1], corpus.at[step, 3], send_b.at[step], recv_b.at[step], other)
+
+    def ends(h):
+        part = pl.ds(h * piece, piece)
+        return (
+            remote(
+                corpus.at[last - 2, 0, part], corpus.at[last, 0, part],
+                send_r.at[last + h], recv_r.at[last + h], right,
+            ),
+            remote(
+                corpus.at[last - 2, 1, part], corpus.at[last, 1, part],
+                send_l.at[last + h], recv_l.at[last + h], left,
+            ),
+        )
+
+    def ends_across(h):
+        part = pl.ds(h * piece, piece)
+        return (
+            remote(
+                corpus.at[last, 0, part], corpus.at[last, 2, part],
+                send_a.at[last + h], recv_a.at[last + h], other,
+            ),
+            remote(
+                corpus.at[last, 1, part], corpus.at[last, 3, part],
+                send_b.at[last + h], recv_b.at[last + h], other,
+            ),
+        )
 
     def blocks_of(step):
         away = (step + 1) // 2
@@ -155,6 +183,8 @@
         pltpu.make_async_copy(passages.at[1], corpus.at[0, 0], load_sem.at[0]),
         pltpu.make_async_copy(passages.at[0], corpus.at[0, 1], load_sem.at[1]),
         pltpu.make_async_copy(queries_in, queries, load_sem.at[2]),
+        pltpu.make_async_copy(first_in, first, load_sem.at[3]),
+        pltpu.make_async_copy(followup_in, followup, load_sem.at[4]),
     )
     for load in loads:
         load.start()
@@ -180,24 +210,24 @@
     total[...] = jnp.zeros_like(total)
     for j in range(top):
         asked[j] = jnp.broadcast_to(first[j : j + 1, :].astype(jnp.float32), (size, rows)).T
-        chosen[j] = jnp.broadcast_to(followup[j : j + 1, :].astype(jnp.float32), (size, rows))
+        chosen[j] = jnp.broadcast_to(followup[j : j + 1, :].astype(jnp.float32), (size, rows)).T
     picked[...] = jnp.zeros_like(picked)
-
-    def absorb(step, slot, carry):
+    lane = lax.broadcasted_iota(jnp.int32, (1, size), 1)
+
+    def absorb(sources, place, names, carry):
         peak, norm = carry
-        place = pl.ds(slot * size, 2 * size)
-        for t in (slot, slot + 1):
-            high, low = halves(corpus[step, t])
-            corpus_hi[step, pl.ds(t * size, size), :] = high
-            corpus_lo[step, pl.ds(t * size, size), :] = low
-        both = dot_nt(pair[...], corpus_hi[step, place, :])
+        split = [halves(source[...]) for source in sources]
+        high = jnp.concatenate([h for h, _ in split], axis=0)
+        low = jnp.concatenate([l for _, l in split], axis=0)
+        place[0][...] = high.T
+        place[1][...] = low.T
+        both = dot_nn(pair[...], place[0][...])
         found = SOFTMAX_HEAT * (
-            both[:rows] + both[rows:] + dot_nt(pair[pl.ds(0, rows), :], corpus_lo[step, place, :])
+            both[:rows] + both[rows:] + dot_nn(pair[pl.ds(0, rows), :], place[1][...])
         )
         parts, hits = [], []
         top_score = peak
-        for t, block in enumerate(blocks_of(step)[slot : slot + 2]):
-            name = block.astype(jnp.float32)
+        for t, name in enumerate(names):
             hit = asked[0] == name
             for j in range(1, top):
                 hit = jnp.logical_or(hit, asked[j] == name)
@@ -210,12 +240,26 @@
             [jnp.where(hit, jnp.exp(part - top_score), 0.0) for hit, part in zip(hits, parts)], axis=1
         )
         norm = norm * shrink + jnp.sum(weights, axis=1, keepdims=True)
-        high, low = halves(weights)
-        mixed = dot_nn(jnp.concatenate([high, low], axis=0), corpus_hi[step, place, :])
-        total[...] = total[...] * shrink + (
-            mixed[:rows] + mixed[rows:] + dot_nn(high, corpus_lo[step, place, :])
-        )
+        first_half, second_half = halves(weights)
+        mixed = dot_nn(jnp.concatenate([first_half, second_half], axis=0), high)
+        total[...] = total[...] * shrink + (mixed[:rows] + mixed[rows:] + dot_nn(first_half, low))
         return top_score, norm
+
+    def whole(step, slot, carry):
+        sources = [corpus.at[step, t] for t in (slot, slot + 1)]
+        place = (turned_hi.at[step, slot // 2], turned_lo.at[step, slot // 2])
+        names = [block.astype(jnp.float32) for block in blocks_of(step)[slot : slot + 2]]
+        return absorb(sources, place, names, carry)
+
+    def partial(h, slot, carry):
+        sources = [corpus.at[last, t, pl.ds(h * piece, piece)] for t in (slot, slot + 1)]
+        spread = pl.ds(h * size, size)
+        place = (
+            turned_hi.at[last, slot // 2, :, spread],
+            turned_lo.at[last, slot // 2, :, spread],
+        )
+        a, b = (block.astype(jnp.float32) for block in blocks_of(last)[slot : slot + 2])
+        return absorb(sources, place, [jnp.where(lane < piece, a, b)], carry)
 
     def first_round(step, carry):
         @pl.when(step > 0)
@@ -223,40 +267,69 @@
             rightward(step, corpus.at[step, 0]).wait_recv()
             leftward(step, corpus.at[step, 1]).wait_recv()
 
-        @pl.when(step < chips - 2)
+        @pl.when(step < last - 2)
         def _():
             rightward(step + 2, corpus.at[step, 0]).start()
             leftward(step + 2, corpus.at[step, 1]).start()
 
+        @pl.when(step == last - 2)
+        def _():
+            for h in range(2):
+                for copy in ends(h):
+                    copy.start()
+
         across_a(step).start()
         across_b(step).start()
-        carry = absorb(step, 0, carry)
+        carry = whole(step, 0, carry)
         across_a(step).wait_recv()
         across_b(step).wait_recv()
-        return absorb(step, 2, carry)
-
-    start = (jnp.full((rows, 1), MASKED, jnp.float32), jnp.zeros((rows, 1), jnp.float32))
-    _, norm = lax.fori_loop(0, chips, first_round, start)
+        return whole(step, 2, carry)
+
+    carry = (jnp.full((rows, 1), MASKED, jnp.float32), jnp.zeros((rows, 1), jnp.float32))
+    carry = lax.fori_loop(0, last, first_round, carry)
+    for h in range(2):
+        for copy in ends(h):
+            copy.wait_recv()
+        for copy in ends_across(h):
+            copy.start()
+        carry = partial(h, 0, carry)
+        for copy in ends_across(h):
+            copy.wait_recv()
+        carry = partial(h, 2, carry)
+    norm = carry[1]
 
     after = queries[...] + (FEEDBACK * width ** (-0.5)) * (total[...] / norm)
     expanded[...] = after
     put_pair(after)
 
+    def score(step, s):
+        both = dot_nn(pair[...], turned_hi[step, s])
+        return both[:rows] + both[rows:] + dot_nn(pair[pl.ds(0, rows), :], turned_lo[step, s])
+
+    def pick(values, names):
+        for j in range(top):
+            value = picked[j]
+            for name, found in zip(names, values):
+                value = jnp.where(chosen[j] == name, found, value)
+            picked[j] = value
+
     def second_round(step, carry):
-        both = dot_nt(corpus_hi[step], pair[...])
-        found = both[:, :rows] + both[:, rows:] + dot_nt(corpus_lo[step], pair[pl.ds(0, rows), :])
         ids = [block.astype(jnp.float32) for block in blocks_of(step)]
-        for j in range(top):
-            names = chosen[j]
-            value = picked[j]
-            for t in range(4):
-                value = jnp.where(names == ids[t], found[t * size : (t + 1) * size, :], value)
-            picked[j] = value
+        for s in range(2):
+            found = score(step, s)
+            pick([found[:, :size], found[:, size:]], ids[2 * s : 2 * s + 2])
         return carry
 
-    lax.fori_loop(0, chips, second_round, 0)
+    lax.fori_loop(0, last, second_round, 0)
+    ids = [block.astype(jnp.float32) for block in blocks_of(last)]
+    for s in range(2):
+        found = score(last, s)
+        a, b = found[:, :size], found[:, size:]
+        early = jnp.where(lane < piece, a, pltpu.roll(b, piece, 1))
+        late = jnp.where(lane < piece, pltpu.roll(a, piece, 1), b)
+        pick([early, late], ids[2 * s : 2 * s + 2])
     for j in range(top):
-        scores[:, j, :] = picked[j].T
+        scores[:, j, :] = picked[j]
 
     def drain(step, carry):
         @pl.when(step > 0)
@@ -268,7 +341,10 @@
         across_b(step).wait_send()
         return carry
 
-    lax.fori_loop(0, chips, drain, 0)
+    lax.fori_loop(0, last, drain, 0)
+    for h in range(2):
+        for copy in ends(h) + ends_across(h):
+            copy.wait_send()
 
 
 def grant_of(queries, passages, first_blocks):
@@ -300,25 +376,27 @@
             jax.ShapeDtypeStruct((rows, width), jnp.float32),
             jax.ShapeDtypeStruct((rows, top, size), jnp.float32),
         ),
-        in_specs=[hbm, hbm, vmem, vmem],
+        in_specs=[hbm, hbm, hbm, hbm],
         out_specs=(vmem, vmem),
         scratch_shapes=[
+            pltpu.VMEM((top, rows), jnp.int32),
+            pltpu.VMEM((top, rows), jnp.int32),
             pltpu.VMEM((chips, 4, size, width), jnp.float32),
-            pltpu.VMEM((chips, 4 * size, width), jnp.bfloat16),
-            pltpu.VMEM((chips, 4 * size, width), jnp.bfloat16),
+            pltpu.VMEM((chips, 2, width, 2 * size), jnp.bfloat16),
+            pltpu.VMEM((chips, 2, width, 2 * size), jnp.bfloat16),
             pltpu.VMEM((rows, width), jnp.float32),
             pltpu.VMEM((2 * rows, width), jnp.bfloat16),
             pltpu.VMEM((rows, width), jnp.float32),
             pltpu.VMEM((top, rows, size), jnp.float32),
-            pltpu.VMEM((top, size, rows), jnp.float32),
-            pltpu.VMEM((top, size, rows), jnp.float32),
-            pltpu.SemaphoreType.DMA((3,)),
+            pltpu.VMEM((top, rows, size), jnp.float32),
+            pltpu.VMEM((top, rows, size), jnp.float32),
+            pltpu.SemaphoreType.DMA((5,)),
         ]
-        + [pltpu.SemaphoreType.DMA((chips,))] * 8,
+        + [pltpu.SemaphoreType.DMA((chips + 1,))] * 8,
         compiler_params=pltpu.CompilerParams(
             collective_id=0, has_side_effects=True, vmem_limit_bytes=VMEM_BYTES
         ),
-    )(queries, passages, first_blocks.T, followup_blocks.T)
+    )(*[pltpu.with_memory_space_constraint(x, pltpu.HBM) for x in (queries, passages, first_blocks.T, followup_blocks.T)])
 
 
 def solution(mesh):

time: 99.3 us -> 94.7 us (0.954)
  Pallas kernels: 95.8 us -> 92.5 us
  local copies, waits for them, and re-layouts: 2.63 us -> 1.5 us
    pallas_call x1, Pallas kernels: 95.8 us -> 92.5 us  [device_program(): pl.pallas_call(functools.partial(ring_kernel, chips), out_shape=(jax.Shap...]
    unnamed x4 -> x2, local copies, waits for them, and re-layouts: 2.63 us -> 1.5 us
where the time goes in v1:
time: 94.7 us; the launch traced here: 94.6 us
  Pallas kernels  92.5 us (98%)
  local copies, waits for them, and re-layouts  1.5 us (2%)
    pallas_call x1, Pallas kernels, device_program(): pl.pallas_call(functools.partial(ring_kernel, chips), out_shape=(jax.Shap...  92.5 us

profile of v1, /device:TPU:1, one launch (start us, length us, event | category | flops | bytes accessed | tf_op | source)
XLA Modules:
  0.0 94.6 jit_solution(9754420586423935113)
XLA Ops:
  0.6 92.5 %shard_map.59 = (f32[128,1024]{1,0:T(8,128)S(1)}, f32[128,4,128]{2,1,0:T(4,128)S(1)}) custom-call(f32[128,1024]{1,0:T(8,128)} %queries_in.1, f32[2,128,1024]{2,1,0:T(8,128)} %passages.1, s32[4,128]{1,0:T(4,128)} %bitcast.2, s32[4,128]{1,0:T(4,128)} %bitcast.3), custom_call_target="tpu_custom_call" | custom-call | tf_op jit(solution)/shard_map/pallas_call | solution.py:373
  93.1 0.8 copy.8
  93.9 0.7 copy.9

commit v2 on v0

v2 whole, which is shorter than its diff:
```python
import functools

import jax
import jax.numpy as jnp
from jax import lax
from jax.experimental import pallas as pl
from jax.experimental.pallas import tpu as pltpu
from jax.sharding import PartitionSpec as P

SOFTMAX_HEAT = 2.0
FEEDBACK = 0.5
MASKED = -1e30
VMEM_BYTES = 50 * 1024 * 1024


def position_targets(block_ids, capacity):
    flat_ids = block_ids.reshape(-1)
    matches = flat_ids[:, None] == flat_ids[None, :]
    positions = jnp.arange(flat_ids.shape[0], dtype=jnp.int32)
    earlier = positions[None, :] < positions[:, None]
    ranking = jnp.sum(jnp.logical_and(matches, earlier), axis=1, dtype=jnp.int32)
    return flat_ids * capacity + ranking


def pack_rows(values, targets, owners, resident_blocks, capacity):
    buffer = jnp.zeros((owners * resident_blocks * capacity, values.shape[1]), values.dtype)
    buffer = buffer.at[targets].set(values)
    return buffer.reshape(owners, resident_blocks, capacity, values.shape[1])


def reply(results):
    return (
        lax.all_to_all(results[0], "cluster", split_axis=0, concat_axis=0, tiled=True),
        lax.all_to_all(results[1], "cluster", split_axis=0, concat_axis=0, tiled=True),
        lax.all_to_all(results[2], "cluster", split_axis=0, concat_axis=0, tiled=True),
    )


def send_back(match_scores):
    return lax.all_to_all(match_scores, "cluster", split_axis=0, concat_axis=0, tiled=True)


def local(queries, passages, first_blocks, followup_blocks):
    owners = lax.axis_size("cluster")
    resident_blocks = passages.shape[0]
    embed_width = queries.shape[1]
    per_query = first_blocks.shape[1]
    pair_count = queries.shape[0] * per_query
    all_blocks = owners * resident_blocks
    capacity = max(2, (3 * pair_count + 2 * all_blocks - 1) // (2 * all_blocks))
    coefficient = FEEDBACK * embed_width ** (-0.5)
    highest = lax.Precision.HIGHEST

    def project_onto_centroid(arrived):
        return jnp.einsum("nbce,bre->nbcr", arrived, passages, precision=highest)

    first_targets = position_targets(first_blocks, capacity)
    second_targets = position_targets(followup_blocks, capacity)
    repeated = jnp.repeat(queries, per_query, axis=0)
    first_sent = pack_rows(repeated, first_targets, owners, resident_blocks, capacity)
    match_scores = SOFTMAX_HEAT * project_onto_centroid(
        lax.all_to_all(first_sent, "cluster", split_axis=0, concat_axis=0, tiled=True)
    )
    highs = jnp.max(match_scores, axis=3)
    weights = jnp.exp(match_scores - highs[..., None])
    totals = jnp.sum(weights, axis=3)
    vectors = jnp.einsum("nbcr,bre->nbce", weights, passages, precision=highest)
    highs, totals, vectors = reply((highs, totals, vectors))
    highs = highs.reshape(-1)[first_targets].reshape(-1, per_query)
    totals = totals.reshape(-1)[first_targets].reshape(-1, per_query)
    vectors = vectors.reshape(-1, embed_width)[first_targets].reshape(-1, per_query, embed_width)
    peak_high = jnp.max(highs, axis=1, keepdims=True)
    scaled = jnp.exp(highs - peak_high)
    denominator = jnp.sum(scaled * totals, axis=1)
    feedback = jnp.einsum("qk,qke->qe", scaled, vectors, precision=highest) / denominator[:, None]
    expanded = queries + coefficient * feedback
    expanded_sent = pack_rows(
        jnp.repeat(expanded, per_query, axis=0), second_targets, owners, resident_blocks, capacity
    )
    returned = (lambda arrived: send_back(project_onto_centroid(arrived)))(
        lax.all_to_all(expanded_sent, "cluster", split_axis=0, concat_axis=0, tiled=True)
    )
    second_scores = returned.reshape(-1, returned.shape[3])[second_targets].reshape(
        queries.shape[0], per_query, -1
    )
    return (expanded, second_scores)


def dot_nt(a, b):
    return lax.dot_general(a, b, (((1,), (1,)), ((), ())), preferred_element_type=jnp.float32)


def dot_nn(a, b):
    return lax.dot_general(a, b, (((1,), (0,)), ((), ())), preferred_element_type=jnp.float32)


def halves(x):
    high = x.astype(jnp.bfloat16)
    return high, (x - high.astype(jnp.float32)).astype(jnp.bfloat16)


def hub_kernel(
    queries_in, passages, first_in, followup_in, expanded, scores,
    first, followup, corpus, turned_hi, turned_lo, queries, pair, total, asked, chosen, picked,
    expanded_out, scores_out,
    load_sem, send_c, recv_c, send_y, recv_y, send_z, recv_z, send_x, recv_x, send_back, recv_back,
):
    me = lax.axis_index("cluster")
    core, y, z = me % 2, (me // 2) % 2, me // 4
    rows, width = expanded.shape
    both_rows = 2 * rows
    top, _, size = asked.shape
    piece = size // 2
    inner = ((z + 1) % 4) // 2
    mate_z = z + 1 - 2 * (z % 2)
    far_z = 3 - z
    far_mate_z = far_z + 1 - 2 * (far_z % 2)

    def device(zz, yy, cc):
        return (2 * zz + yy) * 2 + cc

    mate = device(mate_z, y, core)
    beside = device(z, 1 - y, core)
    far = device(far_z, y, core)
    other = device(z, y, 1 - core)

    plan = (
        (z, y, 0), (z, y, 1),
        (mate_z, y, 0), (mate_z, y, 1), (mate_z, 1 - y, 1), (mate_z, 1 - y, 0),
        (z, 1 - y, 0), (z, 1 - y, 1), (far_z, 1 - y, 0), (far_z, 1 - y, 1), (far_mate_z, 1 - y, 0),
        (far_z, y, 0), (far_z, y, 1), (far_mate_z, y, 0), (far_mate_z, y, 1), (far_mate_z, 1 - y, 1),
    )

    def names_of(unit):
        chip, index = 0, 0
        for k, (zz, yy, ii) in enumerate(plan):
            here = jnp.int32(unit == k) if isinstance(unit, int) else (unit == k).astype(jnp.int32)
            chip = chip + here * (2 * zz + yy)
            index = index + here * ii
        return (
            ((2 * chip + core) * 2 + index).astype(jnp.float32),
            ((2 * chip + 1 - core) * 2 + index).astype(jnp.float32),
        )

    def remote(src, dst, send, recv, target):
        return pltpu.make_async_remote_copy(
            src_ref=src, dst_ref=dst, send_sem=send, recv_sem=recv,
            device_id={"cluster": target}, device_id_type=pl.DeviceIdType.MESH,
        )

    def part(h):
        return pl.ds(h * piece, piece)

    def unit_copy(source, unit, sems, k, target):
        return remote(corpus.at[source, 0], corpus.at[unit, 0], sems[0].at[k], sems[1].at[k], target)

    def half_copy(source, unit, h, sems, k, target):
        return remote(
            corpus.at[source, 0, part(h)], corpus.at[unit, 0, part(h)],
            sems[0].at[k], sems[1].at[k], target,
        )

    on_c, on_y, on_z, on_x = (send_c, recv_c), (send_y, recv_y), (send_z, recv_z), (send_x, recv_x)

    def ids_up(k):
        held = (first, followup)[k]
        return remote(held.at[0], held.at[1], send_c.at[k], recv_c.at[k], mate)

    def queries_up():
        return remote(
            queries.at[pl.ds(0, rows)], queries.at[pl.ds(rows, rows)], send_c.at[2], recv_c.at[2], mate
        )

    def up(unit, h):
        source = unit - 2 if isinstance(unit, int) and unit < 4 else unit
        return half_copy(source, unit, h, on_c, 2 * unit + h, mate)

    def side(unit):
        return unit_copy(unit - 3 if isinstance(unit, int) and unit > 7 else unit, unit, on_y, unit, beside)

    def across(unit):
        return remote(corpus.at[unit, 0], corpus.at[unit, 1], send_x.at[unit], recv_x.at[unit], other)

    def across_half(unit, h):
        k = 16 + (unit // 5 - 1) * 2 + h
        return remote(
            corpus.at[unit, 0, part(h)], corpus.at[unit, 1, part(h)], send_x.at[k], recv_x.at[k], other
        )

    def back(k):
        source, target = ((expanded_out, expanded), (scores_out, scores))[k]
        return remote(source, target, send_back.at[k], recv_back.at[k], mate)

    loads = (
        pltpu.make_async_copy(passages.at[0], corpus.at[0, 0], load_sem.at[0]),
        pltpu.make_async_copy(passages.at[1], corpus.at[1, 0], load_sem.at[1]),
        pltpu.make_async_copy(queries_in, queries.at[pl.ds(0, rows)], load_sem.at[2]),
        pltpu.make_async_copy(first_in, first.at[0], load_sem.at[3]),
        pltpu.make_async_copy(followup_in, followup.at[0], load_sem.at[4]),
    )
    for load in loads:
        load.start()
    barrier = pltpu.get_barrier_semaphore()
    for target in (mate, beside, other):
        pl.semaphore_signal(
            barrier, inc=1, device_id={"cluster": target}, device_id_type=pl.DeviceIdType.MESH
        )

    @pl.when(inner == 1)
    def _():
        pl.semaphore_signal(
            barrier, inc=1, device_id={"cluster": far}, device_id_type=pl.DeviceIdType.MESH
        )

    pl.semaphore_wait(barrier, 3 + inner)
    for load in loads:
        load.wait()

    @pl.when(inner == 0)
    def _():
        ids_up(0).start()
        ids_up(1).start()
        queries_up().start()
        corner_side = [
            remote(corpus.at[k, 0], corpus.at[5 - k, 0], send_y.at[k], recv_y.at[k], beside)
            for k in (1, 0)
        ]
        for copy in corner_side:
            copy.start()
        for unit in (2, 3):
            for h in range(2):
                up(unit, h).start()
        for copy, unit in zip(corner_side, (4, 5)):
            copy.wait_recv()
            for h in range(2):
                up(unit, h).start()
        for k in range(2):
            back(k).wait_recv()
        ids_up(0).wait_send()
        ids_up(1).wait_send()
        queries_up().wait_send()
        for copy in corner_side:
            copy.wait_send()
        for unit in (2, 3, 4, 5):
            for h in range(2):
                up(unit, h).wait_send()

    @pl.when(inner == 1)
    def _():
        hub(
            first, followup, corpus, turned_hi, turned_lo, queries, pair, total, asked, chosen,
            picked, expanded, scores, expanded_out, scores_out,
            names_of, unit_copy, half_copy, ids_up, queries_up, across, across_half, back, part,
            on_c, on_y, on_z, mate, beside, far,
        )


def hub(
    first, followup, corpus, turned_hi, turned_lo, queries, pair, total, asked, chosen,
    picked, expanded, scores, expanded_out, scores_out,
    names_of, unit_copy, half_copy, ids_up, queries_up, across, across_half, back, part,
    on_c, on_y, on_z, mate, beside, far,
):
    rows, width = expanded.shape
    both_rows = 2 * rows
    top, _, size = asked.shape
    piece = size // 2
    lane = lax.broadcasted_iota(jnp.int32, (1, size), 1)

    def from_mate(unit, h):
        return half_copy(unit, unit, h, on_c, 2 * unit + h, mate)

    def from_side(t):
        return unit_copy(5 + t, 5 + t, on_y, 5 + t, beside)

    def last_side(h):
        return half_copy(13, 10, h, on_y, 10 + h, beside)

    def own_side(k):
        return unit_copy(k, 6 + k, on_y, 6 + k, beside)

    def pass_side(t):
        return unit_copy(10 + t, 7 + t, on_y, 7 + t, beside)

    def own_far(k):
        return unit_copy(k, 11 + k, on_z, k, far)

    def pass_far(t, h):
        return half_copy(t, 11 + t, h, on_z, 2 * t + h, far)

    def from_far(t):
        return unit_copy(10 + t, 10 + t, on_z, t - 1, far)

    def from_far_half(t, h):
        return half_copy(10 + t, 10 + t, h, on_z, 2 * (t - 1) + h, far)

    for k in range(2):
        own_far(k).start()
        own_side(k).start()
    for k in range(2):
        across(k).start()
    from_far(1).wait_recv()
    pass_side(1).start()
    across(11).start()
    from_side(1).wait_recv()
    across(6).start()
    for k in range(2):
        ids_up(k).wait_recv()
    queries_up().wait_recv()

    def put_pair(x):
        high, low = halves(x)
        pair[pl.ds(0, both_rows), :] = high
        pair[pl.ds(both_rows, both_rows), :] = low

    def dot_three(high, low, right_high, right_low):
        return dot_nn(high, right_high) + (dot_nn(low, right_high) + dot_nn(high, right_low))

    put_pair(queries[...])
    total[...] = jnp.zeros_like(total)
    picked[...] = jnp.zeros_like(picked)
    for g in range(2):
        group = pl.ds(g * rows, rows)
        for j in range(top):
            for held, spread in ((first, asked), (followup, chosen)):
                line = held[g, j : j + 1, :].astype(jnp.float32)
                spread[j, group, :] = jnp.broadcast_to(line, (size, rows)).T

    def absorb(pieces, carry):
        peak, norm = carry
        highs, lows, names = [], [], []
        for unit, h in pieces:
            high, low = halves(
                jnp.concatenate([corpus[unit, 0, part(h), :], corpus[unit, 1, part(h), :]], axis=0)
            )
            place = pl.ds(h * size, size)
            turned_hi[unit, :, place] = high.T
            turned_lo[unit, :, place] = low.T
            highs.append(high)
            lows.append(low)
            own, others = names_of(unit)
            names.append(jnp.where(lane < piece, own, others))
        wide = [
            jnp.concatenate([turned[unit, :, pl.ds(h * size, size)] for unit, h in pieces], axis=1)
            for turned in (turned_hi, turned_lo)
        ]
        all_found = dot_three(
            pair[pl.ds(0, both_rows), :], pair[pl.ds(both_rows, both_rows), :], *wide
        )
        sums = [all_found[:, k * size : (k + 1) * size] for k in range(len(pieces))]
        parts, hits = [], []
        top_score = peak
        for name, found in zip(names, sums):
            hit = asked[0] == name
            for j in range(1, top):
                hit = jnp.logical_or(hit, asked[j] == name)
            score = jnp.where(hit, SOFTMAX_HEAT * found, MASKED)
            top_score = jnp.maximum(top_score, jnp.max(score, axis=1, keepdims=True))
            parts.append(score)
            hits.append(hit)
        shrink = jnp.exp(peak - top_score)
        weights = jnp.concatenate(
            [jnp.where(hit, jnp.exp(score - top_score), 0.0) for hit, score in zip(hits, parts)], axis=1
        )
        norm = norm * shrink + jnp.sum(weights, axis=1, keepdims=True)
        weight_high, weight_low = halves(weights)
        mixed = dot_three(
            weight_high, weight_low, jnp.concatenate(highs, axis=0), jnp.concatenate(lows, axis=0)
        )
        total[...] = total[...] * shrink + mixed
        return top_score, norm

    def take(unit, carry):
        across(unit).wait_recv()
        return absorb([(unit, 0), (unit, 1)], carry)

    def step(t, carry):
        carry = take(4 + t, carry)
        carry = take(t - 1, carry)
        from_mate(t, 0).wait_recv()

        @pl.when(t < 5)
        def _():
            pass_far(t, 0).start()

        carry = take(9 + t, carry)

        @pl.when(t < 5)
        def _():
            from_mate(t, 1).wait_recv()
            pass_far(t, 1).start()
            across(t).start()
            from_side(t).wait_recv()
            across(5 + t).start()

            @pl.when(t == 2)
            def _():
                from_far(t).wait_recv()
                pass_side(t).start()

            @pl.when(t > 2)
            def _():
                for h in range(2):
                    from_far_half(t, h).wait_recv()

            across(10 + t).start()

            @pl.when(t == 3)
            def _():
                for h in range(2):
                    last_side(h).start()

        return carry

    carry = (
        jnp.full((both_rows, 1), MASKED, jnp.float32), jnp.zeros((both_rows, 1), jnp.float32)
    )
    carry = take(0, carry)
    carry = lax.fori_loop(2, 6, step, carry)

    def finish(h, carry):
        @pl.when(h == 1)
        def _():
            from_mate(5, h).wait_recv()

        across_half(5, h).start()
        last_side(h).wait_recv()
        across_half(10, h).start()
        from_far_half(5, h).wait_recv()
        across_half(15, h).start()
        for unit in (5, 10, 15):
            across_half(unit, h).wait_recv()
        return absorb([(5, h), (10, h), (15, h)], carry)

    _, norm = lax.fori_loop(0, 2, finish, carry)

    after = queries[...] + (FEEDBACK * width ** (-0.5)) * (total[...] / norm)
    expanded_out[...] = after[rows:]
    expanded[...] = after[:rows]
    put_pair(after)
    back(0).start()

    def second_round(unit, carry):
        found = dot_three(
            pair[pl.ds(0, both_rows), :], pair[pl.ds(both_rows, both_rows), :],
            turned_hi[unit], turned_lo[unit],
        )
        a, b = found[:, :size], found[:, size:]
        own = jnp.where(lane < piece, a, pltpu.roll(b, piece, 1))
        others = jnp.where(lane < piece, pltpu.roll(a, piece, 1), b)
        names = names_of(unit)
        for j in range(top):
            value = jnp.where(chosen[j] == names[0], own, picked[j])
            picked[j] = jnp.where(chosen[j] == names[1], others, value)
        return carry

    lax.fori_loop(0, 16, second_round, 0)
    for j in range(top):
        scores_out[:, j, :] = picked[j, pl.ds(rows, rows), :]
    for j in range(top):
        scores[:, j, :] = picked[j, pl.ds(0, rows), :]
    back(1).start()

    for k in range(2):
        own_far(k).wait_send()
        own_side(k).wait_send()
        pass_side(1 + k).wait_send()
        last_side(k).wait_send()
        back(k).wait_send()

    def drain(t, carry):
        for h in range(2):
            pass_far(t, h).wait_send()
        return carry

    lax.fori_loop(2, 5, drain, 0)

    def drain_across(unit, carry):
        @pl.when(unit % 5 != 0)
        def _():
            across(unit).wait_send()

        return carry

    across(0).wait_send()
    lax.fori_loop(1, 15, drain_across, 0)
    for unit in (5, 10, 15):
        for h in range(2):
            across_half(unit, h).wait_send()


def grant_of(queries, passages, first_blocks):
    resident, size, width = passages.shape
    rows = queries.shape[0]
    corpus = lax.axis_size("cluster") * resident * size * width * 8
    return corpus + (12 * rows * width + 10 * first_blocks.shape[1] * rows * size) * 4


def hub_fits(queries, passages, first_blocks):
    owners = lax.axis_size("cluster")
    resident, size, _ = passages.shape
    fits = grant_of(queries, passages, first_blocks) < VMEM_BYTES
    return owners == 16 and resident == 2 and fits and queries.shape[0] == size


def device_program(queries, passages, first_blocks, followup_blocks):
    if not hub_fits(queries, passages, first_blocks):
        return local(queries, passages, first_blocks, followup_blocks)
    units = lax.axis_size("cluster")
    rows, width = queries.shape
    size = passages.shape[1]
    top = first_blocks.shape[1]
    vmem = pl.BlockSpec(memory_space=pltpu.VMEM)
    hbm = pl.BlockSpec(memory_space=pltpu.HBM)
    operands = (queries, passages, first_blocks.T, followup_blocks.T)
    dma = pltpu.SemaphoreType.DMA
    return pl.pallas_call(
        hub_kernel,
        out_shape=(
            jax.ShapeDtypeStruct((rows, width), jnp.float32),
            jax.ShapeDtypeStruct((rows, top, size), jnp.float32),
        ),
        in_specs=[hbm, hbm, hbm, hbm],
        out_specs=(vmem, vmem),
        scratch_shapes=[
            pltpu.VMEM((2, top, rows), jnp.int32),
            pltpu.VMEM((2, top, rows), jnp.int32),
            pltpu.VMEM((units, 2, size, width), jnp.float32),
            pltpu.VMEM((units, width, 2 * size), jnp.bfloat16),
            pltpu.VMEM((units, width, 2 * size), jnp.bfloat16),
            pltpu.VMEM((2 * rows, width), jnp.float32),
            pltpu.VMEM((4 * rows, width), jnp.bfloat16),
            pltpu.VMEM((2 * rows, width), jnp.float32),
            pltpu.VMEM((top, 2 * rows, size), jnp.float32),
            pltpu.VMEM((top, 2 * rows, size), jnp.float32),
            pltpu.VMEM((top, 2 * rows, size), jnp.float32),
            pltpu.VMEM((rows, width), jnp.float32),
            pltpu.VMEM((rows, top, size), jnp.float32),
            dma((5,)),
            dma((12,)), dma((12,)),
            dma((12,)), dma((12,)),
            dma((10,)), dma((10,)),
            dma((22,)), dma((22,)),
            dma((2,)), dma((2,)),
        ],
        compiler_params=pltpu.CompilerParams(
            collective_id=0, has_side_effects=True, vmem_limit_bytes=VMEM_BYTES
        ),
    )(*[pltpu.with_memory_space_constraint(x, pltpu.HBM) for x in operands])


def solution(mesh):
    return jax.shard_map(
        device_program,
        mesh=mesh,
        in_specs=(
            P(("parts", "cluster"), None),
            P(("parts", "cluster"), None, None),
            P(("parts", "cluster"), None),
            P(("parts", "cluster"), None),
        ),
        out_specs=(P(("parts", "cluster"), None), P(("parts", "cluster"), None, None)),
        check_vma=False,
    )
```

time: 99.3 us -> 90.2 us (0.908)
  Pallas kernels: 95.8 us -> 87.9 us
  local copies, waits for them, and re-layouts: 2.63 us -> 1.5 us
    pallas_call x1, Pallas kernels: 95.8 us -> 87.9 us  [device_program(): pl.pallas_call(hub_kernel, out_shape=(jax.ShapeDtypeStruct((rows, width),...]
    unnamed x4 -> x2, local copies, waits for them, and re-layouts: 2.63 us -> 1.5 us
where the time goes in v2:
time: 90.2 us; the launch traced here: 90.1 us
  Pallas kernels  87.9 us (97%)
  local copies, waits for them, and re-layouts  1.5 us (2%)
    pallas_call x1, Pallas kernels, device_program(): pl.pallas_call(hub_kernel, out_shape=(jax.ShapeDtypeStruct((rows, width),...  87.9 us

profile of v2, /device:TPU:1, one launch (start us, length us, event | category | flops | bytes accessed | tf_op | source)
XLA Modules:
  0.0 90.1 jit_solution(14780674815215978858)
XLA Ops:
  0.6 87.9 %shard_map.59 = (f32[128,1024]{1,0:T(8,128)S(1)}, f32[128,4,128]{2,1,0:T(4,128)S(1)}) custom-call(f32[128,1024]{1,0:T(8,128)} %queries_in.1, f32[2,128,1024]{2,1,0:T(8,128)} %passages.1, s32[4,128]{1,0:T(4,128)} %bitcast.2, s32[4,128]{1,0:T(4,128)} %bitcast.3), custom_call_target="tpu_custom_call" | custom-call | tf_op jit(solution)/shard_map/pallas_call | solution.py:517
  88.6 0.8 copy.8
  89.4 0.7 copy.9

commit v3 on v2

v3 whole, which is shorter than its diff:
```python
import functools

import jax
import jax.numpy as jnp
from jax import lax
from jax.experimental import pallas as pl
from jax.experimental.pallas import tpu as pltpu
from jax.sharding import PartitionSpec as P

SOFTMAX_HEAT = 2.0
FEEDBACK = 0.5
MASKED = -1e30
VMEM_BYTES = 50 * 1024 * 1024


def position_targets(block_ids, capacity):
    flat_ids = block_ids.reshape(-1)
    matches = flat_ids[:, None] == flat_ids[None, :]
    positions = jnp.arange(flat_ids.shape[0], dtype=jnp.int32)
    earlier = positions[None, :] < positions[:, None]
    ranking = jnp.sum(jnp.logical_and(matches, earlier), axis=1, dtype=jnp.int32)
    return flat_ids * capacity + ranking


def pack_rows(values, targets, owners, resident_blocks, capacity):
    buffer = jnp.zeros((owners * resident_blocks * capacity, values.shape[1]), values.dtype)
    buffer = buffer.at[targets].set(values)
    return buffer.reshape(owners, resident_blocks, capacity, values.shape[1])


def reply(results):
    return (
        lax.all_to_all(results[0], "cluster", split_axis=0, concat_axis=0, tiled=True),
        lax.all_to_all(results[1], "cluster", split_axis=0, concat_axis=0, tiled=True),
        lax.all_to_all(results[2], "cluster", split_axis=0, concat_axis=0, tiled=True),
    )


def send_back(match_scores):
    return lax.all_to_all(match_scores, "cluster", split_axis=0, concat_axis=0, tiled=True)


def local(queries, passages, first_blocks, followup_blocks):
    owners = lax.axis_size("cluster")
    resident_blocks = passages.shape[0]
    embed_width = queries.shape[1]
    per_query = first_blocks.shape[1]
    pair_count = queries.shape[0] * per_query
    all_blocks = owners * resident_blocks
    capacity = max(2, (3 * pair_count + 2 * all_blocks - 1) // (2 * all_blocks))
    coefficient = FEEDBACK * embed_width ** (-0.5)
    highest = lax.Precision.HIGHEST

    def project_onto_centroid(arrived):
        return jnp.einsum("nbce,bre->nbcr", arrived, passages, precision=highest)

    first_targets = position_targets(first_blocks, capacity)
    second_targets = position_targets(followup_blocks, capacity)
    repeated = jnp.repeat(queries, per_query, axis=0)
    first_sent = pack_rows(repeated, first_targets, owners, resident_blocks, capacity)
    match_scores = SOFTMAX_HEAT * project_onto_centroid(
        lax.all_to_all(first_sent, "cluster", split_axis=0, concat_axis=0, tiled=True)
    )
    highs = jnp.max(match_scores, axis=3)
    weights = jnp.exp(match_scores - highs[..., None])
    totals = jnp.sum(weights, axis=3)
    vectors = jnp.einsum("nbcr,bre->nbce", weights, passages, precision=highest)
    highs, totals, vectors = reply((highs, totals, vectors))
    highs = highs.reshape(-1)[first_targets].reshape(-1, per_query)
    totals = totals.reshape(-1)[first_targets].reshape(-1, per_query)
    vectors = vectors.reshape(-1, embed_width)[first_targets].reshape(-1, per_query, embed_width)
    peak_high = jnp.max(highs, axis=1, keepdims=True)
    scaled = jnp.exp(highs - peak_high)
    denominator = jnp.sum(scaled * totals, axis=1)
    feedback = jnp.einsum("qk,qke->qe", scaled, vectors, precision=highest) / denominator[:, None]
    expanded = queries + coefficient * feedback
    expanded_sent = pack_rows(
        jnp.repeat(expanded, per_query, axis=0), second_targets, owners, resident_blocks, capacity
    )
    returned = (lambda arrived: send_back(project_onto_centroid(arrived)))(
        lax.all_to_all(expanded_sent, "cluster", split_axis=0, concat_axis=0, tiled=True)
    )
    second_scores = returned.reshape(-1, returned.shape[3])[second_targets].reshape(
        queries.shape[0], per_query, -1
    )
    return (expanded, second_scores)


def dot_nt(a, b):
    return lax.dot_general(a, b, (((1,), (1,)), ((), ())), preferred_element_type=jnp.float32)


def dot_nn(a, b):
    return lax.dot_general(a, b, (((1,), (0,)), ((), ())), preferred_element_type=jnp.float32)


def halves(x):
    high = x.astype(jnp.bfloat16)
    return high, (x - high.astype(jnp.float32)).astype(jnp.bfloat16)


def tools_of(corpus, turned_hi, turned_lo, pair, total, asked, names_of, part):
    both_rows = total.shape[0]
    top, _, size = asked.shape
    piece = size // 2
    lane = lax.broadcasted_iota(jnp.int32, (1, size), 1)

    def put_pair(x):
        high, low = halves(x)
        pair[pl.ds(0, x.shape[0]), :] = high
        pair[pl.ds(both_rows, x.shape[0]), :] = low

    def spread_out(held, wide, g):
        rows = held.shape[2]
        for j in range(top):
            line = held[g, j : j + 1, :].astype(jnp.float32)
            wide[j, pl.ds(g * rows, rows), :] = jnp.broadcast_to(line, (size, rows)).T

    def absorb(pieces, count, carry):
        peak, norm = carry
        group = pl.ds(0, count)
        highs, lows, names = [], [], []
        for unit, h in pieces:
            high, low = halves(
                jnp.concatenate([corpus[unit, 0, part(h), :], corpus[unit, 1, part(h), :]], axis=0)
            )
            place = pl.ds(h * size, size)
            turned_hi[unit, :, place] = high.T
            turned_lo[unit, :, place] = low.T
            highs.append(high)
            lows.append(low)
            own, others = names_of(unit)
            names.append(jnp.where(lane < piece, own, others))
        wide = [
            jnp.concatenate([turned[unit, :, pl.ds(h * size, size)] for unit, h in pieces], axis=1)
            for turned in (turned_hi, turned_lo)
        ]
        all_found = dot_three(
            pair[group, :], pair[pl.ds(both_rows, count), :], *wide
        )
        sums = [all_found[:, k * size : (k + 1) * size] for k in range(len(pieces))]
        parts, hits = [], []
        top_score = peak
        for name, found in zip(names, sums):
            hit = asked[0, group, :] == name
            for j in range(1, top):
                hit = jnp.logical_or(hit, asked[j, group, :] == name)
            score = jnp.where(hit, SOFTMAX_HEAT * found, MASKED)
            top_score = jnp.maximum(top_score, jnp.max(score, axis=1, keepdims=True))
            parts.append(score)
            hits.append(hit)
        shrink = jnp.exp(peak - top_score)
        weights = jnp.concatenate(
            [jnp.where(hit, jnp.exp(score - top_score), 0.0) for hit, score in zip(hits, parts)], axis=1
        )
        norm = norm * shrink + jnp.sum(weights, axis=1, keepdims=True)
        weight_high, weight_low = halves(weights)
        mixed = dot_three(
            weight_high, weight_low, jnp.concatenate(highs, axis=0), jnp.concatenate(lows, axis=0)
        )
        total[group, :] = total[group, :] * shrink + mixed
        return top_score, norm

    return put_pair, spread_out, absorb


def dot_three(high, low, right_high, right_low):
    return dot_nn(high, right_high) + (dot_nn(low, right_high) + dot_nn(high, right_low))


def nothing_yet(count):
    return jnp.full((count, 1), MASKED, jnp.float32), jnp.zeros((count, 1), jnp.float32)


def hub_kernel(
    queries_in, passages, first_in, followup_in, expanded, scores,
    first, followup, corpus, turned_hi, turned_lo, queries, pair, total, asked, chosen, picked,
    early, stats, scores_out,
    load_sem, send_c, recv_c, send_y, recv_y, send_z, recv_z, send_x, recv_x, send_back, recv_back,
):
    me = lax.axis_index("cluster")
    core, y, z = me % 2, (me // 2) % 2, me // 4
    rows, width = expanded.shape
    both_rows = 2 * rows
    top, _, size = asked.shape
    piece = size // 2
    inner = ((z + 1) % 4) // 2
    mate_z = z + 1 - 2 * (z % 2)
    hub_z = inner * z + (1 - inner) * mate_z
    end_z = inner * mate_z + (1 - inner) * z
    far_hub, far_end = 3 - hub_z, 3 - end_z

    def device(zz, yy, cc):
        return (2 * zz + yy) * 2 + cc

    mate = device(mate_z, y, core)
    beside = device(z, 1 - y, core)
    far = device(3 - z, y, core)
    other = device(z, y, 1 - core)

    plan = (
        (hub_z, y, 0), (hub_z, y, 1),
        (end_z, y, 0), (end_z, y, 1), (end_z, 1 - y, 1), (end_z, 1 - y, 0),
        (hub_z, 1 - y, 0), (hub_z, 1 - y, 1), (far_hub, 1 - y, 0), (far_hub, 1 - y, 1), (far_end, 1 - y, 0),
        (far_hub, y, 0), (far_hub, y, 1), (far_end, y, 0), (far_end, y, 1), (far_end, 1 - y, 1),
    )

    def names_of(unit):
        chip, index = 0, 0
        for k, (zz, yy, ii) in enumerate(plan):
            here = jnp.int32(unit == k) if isinstance(unit, int) else (unit == k).astype(jnp.int32)
            chip = chip + here * (2 * zz + yy)
            index = index + here * ii
        return (
            ((2 * chip + core) * 2 + index).astype(jnp.float32),
            ((2 * chip + 1 - core) * 2 + index).astype(jnp.float32),
        )

    def remote(src, dst, send, recv, target):
        return pltpu.make_async_remote_copy(
            src_ref=src, dst_ref=dst, send_sem=send, recv_sem=recv,
            device_id={"cluster": target}, device_id_type=pl.DeviceIdType.MESH,
        )

    def part(h):
        return pl.ds(h * piece, piece)

    def unit_copy(source, unit, sems, k, target):
        return remote(corpus.at[source, 0], corpus.at[unit, 0], sems[0].at[k], sems[1].at[k], target)

    def half_copy(source, unit, h, sems, k, target):
        return remote(
            corpus.at[source, 0, part(h)], corpus.at[unit, 0, part(h)],
            sems[0].at[k], sems[1].at[k], target,
        )

    on_c, on_y, on_z, on_x = (send_c, recv_c), (send_y, recv_y), (send_z, recv_z), (send_x, recv_x)

    def ids_up(k):
        held = (first, followup)[k]
        return remote(held.at[0], held.at[1], send_c.at[k], recv_c.at[k], mate)

    def queries_up():
        return remote(
            queries.at[pl.ds(0, rows)], queries.at[pl.ds(rows, rows)], send_c.at[2], recv_c.at[2], mate
        )

    def up(unit, h):
        source = unit - 2 if isinstance(unit, int) and unit < 4 else unit
        return half_copy(source, unit, h, on_c, 2 * unit + h, mate)

    def side(unit):
        return unit_copy(unit - 3 if isinstance(unit, int) and unit > 7 else unit, unit, on_y, unit, beside)

    def across(unit):
        return remote(corpus.at[unit, 0], corpus.at[unit, 1], send_x.at[unit], recv_x.at[unit], other)

    def across_half(unit, h):
        k = 16 + (unit // 5 - 1) * 2 + h
        return remote(
            corpus.at[unit, 0, part(h)], corpus.at[unit, 1, part(h)], send_x.at[k], recv_x.at[k], other
        )

    def back(k):
        source, target = (
            (early.at[0], early.at[1]),
            (stats.at[0], stats.at[1]),
            (scores_out, scores),
        )[k]
        return remote(source, target, send_back.at[k], recv_back.at[k], mate)

    def down(unit, h):
        k = 3 + 2 * (unit - 13) + h
        return half_copy(unit, unit, h, (send_back, recv_back), k, mate)

    loads = (
        pltpu.make_async_copy(passages.at[0], corpus.at[0, 0], load_sem.at[0]),
        pltpu.make_async_copy(passages.at[1], corpus.at[1, 0], load_sem.at[1]),
        pltpu.make_async_copy(queries_in, queries.at[pl.ds(0, rows)], load_sem.at[2]),
        pltpu.make_async_copy(first_in, first.at[0], load_sem.at[3]),
        pltpu.make_async_copy(followup_in, followup.at[0], load_sem.at[4]),
    )
    for load in loads:
        load.start()
    barrier = pltpu.get_barrier_semaphore()
    for target in (mate, beside, other):
        pl.semaphore_signal(
            barrier, inc=1, device_id={"cluster": target}, device_id_type=pl.DeviceIdType.MESH
        )

    @pl.when(inner == 1)
    def _():
        pl.semaphore_signal(
            barrier, inc=1, device_id={"cluster": far}, device_id_type=pl.DeviceIdType.MESH
        )

    pl.semaphore_wait(barrier, 3 + inner)
    for load in loads:
        load.wait()

    @pl.when(inner == 0)
    def _():
        ids_up(0).start()
        ids_up(1).start()
        queries_up().start()
        corner_side = [
            remote(corpus.at[k, 0], corpus.at[5 - k, 0], send_y.at[k], recv_y.at[k], beside)
            for k in (1, 0)
        ]
        for copy in corner_side:
            copy.start()
        for unit in (2, 3):
            for h in range(2):
                up(unit, h).start()
        put_pair, spread_out, absorb = tools_of(
            corpus, turned_hi, turned_lo, pair, total, asked, names_of, part
        )
        put_pair(queries[pl.ds(0, rows), :])
        spread_out(first, asked, 0)
        own = pl.ds(0, rows)
        total[own, :] = jnp.zeros((rows, width), jnp.float32)
        for copy, unit in zip(corner_side, (4, 5)):
            copy.wait_recv()
            for h in range(2):
                up(unit, h).start()
        for h in range(2):
            across_half(5, h).start()
        passed = [
            remote(
                corpus.at[source, 0, part(h)], corpus.at[unit, 0, part(h)],
                send_y.at[unit // 5 * 2 + h - 2], recv_y.at[unit // 5 * 2 + h - 2], beside,
            )
            for source, unit in ((13, 10), (14, 15))
            for h in range(2)
        ]

        def share(k):
            passed[k].wait_recv()
            across_half(10 + k // 2 * 5, k % 2).start()

        for k in range(4):
            down(13 + k // 2, k % 2).wait_recv()
            passed[k].start()
            if k > 0:
                share(k - 1)
        share(3)

        def late(h, carry):
            for unit in (5, 10, 15):
                across_half(unit, h).wait_recv()
            return absorb([(5, h), (10, h), (15, h)], rows, carry)

        peak, norm = lax.fori_loop(0, 2, late, nothing_yet(rows))
        for k in range(2):
            back(k).wait_recv()
        early_peak, early_norm = (
            jnp.broadcast_to(stats[1, k, 0:1, :], (size, rows)).T[:, 0:1] for k in range(2)
        )
        top_score = jnp.maximum(peak, early_peak)
        shrink, early_shrink = jnp.exp(peak - top_score), jnp.exp(early_peak - top_score)
        norm = norm * shrink + early_norm * early_shrink
        mixed = total[own, :] * shrink + early[1] * early_shrink
        expanded[...] = queries[own, :] + (FEEDBACK * width ** (-0.5)) * (mixed / norm)
        back(2).wait_recv()
        for copy in passed:
            copy.wait_send()
        for unit in (5, 10, 15):
            for h in range(2):
                across_half(unit, h).wait_send()
        ids_up(0).wait_send()
        ids_up(1).wait_send()
        queries_up().wait_send()
        for copy in corner_side:
            copy.wait_send()
        for unit in (2, 3, 4, 5):
            for h in range(2):
                up(unit, h).wait_send()

    @pl.when(inner == 1)
    def _():
        hub(
            first, followup, corpus, turned_hi, turned_lo, queries, pair, total, asked, chosen,
            picked, expanded, scores, early, stats, scores_out,
            names_of, unit_copy, half_copy, ids_up, queries_up, across, across_half, back, down, part,
            on_c, on_y, on_z, mate, beside, far,
        )


def hub(
    first, followup, corpus, turned_hi, turned_lo, queries, pair, total, asked, chosen,
    picked, expanded, scores, early, stats, scores_out,
    names_of, unit_copy, half_copy, ids_up, queries_up, across, across_half, back, down, part,
    on_c, on_y, on_z, mate, beside, far,
):
    rows, width = expanded.shape
    both_rows = 2 * rows
    top, _, size = asked.shape
    piece = size // 2
    lane = lax.broadcasted_iota(jnp.int32, (1, size), 1)

    def from_mate(unit, h):
        return half_copy(unit, unit, h, on_c, 2 * unit + h, mate)

    def from_side(t):
        return unit_copy(5 + t, 5 + t, on_y, 5 + t, beside)

    def last_side(h):
        return half_copy(13, 10, h, on_y, 10 + h, beside)

    def own_side(k):
        return unit_copy(k, 6 + k, on_y, 6 + k, beside)

    def pass_side(t):
        return unit_copy(10 + t, 7 + t, on_y, 7 + t, beside)

    def own_far(k):
        return unit_copy(k, 11 + k, on_z, k, far)

    def pass_far(t, h):
        return half_copy(t, 11 + t, h, on_z, 2 * t + h, far)

    def from_far(t):
        return unit_copy(10 + t, 10 + t, on_z, t - 1, far)

    def from_far_half(t, h):
        return half_copy(10 + t, 10 + t, h, on_z, 2 * (t - 1) + h, far)

    for k in range(2):
        own_far(k).start()
        own_side(k).start()
    for k in range(2):
        across(k).start()
    from_far(1).wait_recv()
    pass_side(1).start()
    across(11).start()
    from_side(1).wait_recv()
    across(6).start()
    for k in range(2):
        ids_up(k).wait_recv()
    queries_up().wait_recv()

    put_pair, spread_out, absorb = tools_of(
        corpus, turned_hi, turned_lo, pair, total, asked, names_of, part
    )
    put_pair(queries[...])
    total[...] = jnp.zeros_like(total)
    picked[...] = jnp.zeros_like(picked)
    for g in range(2):
        spread_out(first, asked, g)
        spread_out(followup, chosen, g)

    def take(unit, carry):
        across(unit).wait_recv()
        return absorb([(unit, 0), (unit, 1)], both_rows, carry)

    def step(t, carry):
        carry = take(4 + t, carry)
        carry = take(t - 1, carry)

        @pl.when(t < 5)
        def _():
            from_mate(t, 0).wait_recv()
            pass_far(t, 0).start()

            @pl.when(t > 2)
            def _():
                from_far_half(t, 0).wait_recv()
                down(10 + t, 0).start()

        carry = take(9 + t, carry)

        @pl.when(t < 5)
        def _():
            from_mate(t, 1).wait_recv()
            pass_far(t, 1).start()
            across(t).start()

            @pl.when(t == 2)
            def _():
                from_far(t).wait_recv()
                pass_side(t).start()

            @pl.when(t > 2)
            def _():
                from_far_half(t, 1).wait_recv()
                down(10 + t, 1).start()

            across(10 + t).start()
            from_side(t).wait_recv()
            across(5 + t).start()

            @pl.when(t == 3)
            def _():
                for h in range(2):
                    last_side(h).start()

        return carry

    carry = nothing_yet(both_rows)
    carry = take(0, carry)
    carry = lax.fori_loop(2, 6, step, carry)

    early[0] = total[pl.ds(rows, rows), :]
    for k in range(2):
        line = jnp.broadcast_to(carry[k][rows:], (rows, size)).T
        stats[0, k] = line[: stats.shape[2], :]
    back(1).start()
    back(0).start()

    def finish(h, carry):
        from_mate(5, h).wait_recv()
        across_half(5, h).start()
        last_side(h).wait_recv()
        across_half(10, h).start()
        from_far_half(5, h).wait_recv()
        across_half(15, h).start()
        for unit in (5, 10, 15):
            across_half(unit, h).wait_recv()
        return absorb([(5, h), (10, h), (15, h)], both_rows, carry)

    _, norm = lax.fori_loop(0, 2, finish, carry)

    after = queries[...] + (FEEDBACK * width ** (-0.5)) * (total[...] / norm)
    put_pair(after)
    expanded[...] = after[:rows]

    def score_all(g, out):
        group = pl.ds(g * rows, rows)

        def second_round(turn, carry):
            values = [picked[j, group, :] for j in range(top)]
            for k in range(4):
                unit = 4 * turn + k
                found = dot_three(
                    pair[group, :], pair[pl.ds(both_rows + g * rows, rows), :],
                    turned_hi[unit], turned_lo[unit],
                )
                a, b = found[:, :size], found[:, size:]
                own = jnp.where(lane < piece, a, pltpu.roll(b, piece, 1))
                others = jnp.where(lane < piece, pltpu.roll(a, piece, 1), b)
                names = names_of(unit)
                for j in range(top):
                    value = jnp.where(chosen[j, group, :] == names[0], own, values[j])
                    values[j] = jnp.where(chosen[j, group, :] == names[1], others, value)
            for j in range(top):
                picked[j, group, :] = values[j]
            return carry

        lax.fori_loop(0, 4, second_round, 0)
        for j in range(top):
            out[:, j, :] = picked[j, group, :]

    score_all(1, scores_out)
    back(2).start()
    score_all(0, scores)

    for k in range(2):
        own_far(k).wait_send()
        own_side(k).wait_send()
        pass_side(1 + k).wait_send()
        last_side(k).wait_send()
    for k in range(3):
        back(k).wait_send()
    for unit in (13, 14):
        for h in range(2):
            down(unit, h).wait_send()

    def drain(t, carry):
        for h in range(2):
            pass_far(t, h).wait_send()
        return carry

    lax.fori_loop(2, 5, drain, 0)

    def drain_across(unit, carry):
        @pl.when(unit % 5 != 0)
        def _():
            across(unit).wait_send()

        return carry

    across(0).wait_send()
    lax.fori_loop(1, 15, drain_across, 0)
    for unit in (5, 10, 15):
        for h in range(2):
            across_half(unit, h).wait_send()


def grant_of(queries, passages, first_blocks):
    resident, size, width = passages.shape
    rows = queries.shape[0]
    corpus = lax.axis_size("cluster") * resident * size * width * 8
    return corpus + (12 * rows * width + 10 * first_blocks.shape[1] * rows * size) * 4


def hub_fits(queries, passages, first_blocks):
    owners = lax.axis_size("cluster")
    resident, size, _ = passages.shape
    fits = grant_of(queries, passages, first_blocks) < VMEM_BYTES
    return owners == 16 and resident == 2 and fits and queries.shape[0] == size


def device_program(queries, passages, first_blocks, followup_blocks):
    if not hub_fits(queries, passages, first_blocks):
        return local(queries, passages, first_blocks, followup_blocks)
    units = lax.axis_size("cluster")
    rows, width = queries.shape
    size = passages.shape[1]
    top = first_blocks.shape[1]
    vmem = pl.BlockSpec(memory_space=pltpu.VMEM)
    hbm = pl.BlockSpec(memory_space=pltpu.HBM)
    operands = (queries, passages, first_blocks.T, followup_blocks.T)
    dma = pltpu.SemaphoreType.DMA
    return pl.pallas_call(
        hub_kernel,
        out_shape=(
            jax.ShapeDtypeStruct((rows, width), jnp.float32),
            jax.ShapeDtypeStruct((rows, top, size), jnp.float32),
        ),
        in_specs=[hbm, hbm, hbm, hbm],
        out_specs=(vmem, vmem),
        scratch_shapes=[
            pltpu.VMEM((2, top, rows), jnp.int32),
            pltpu.VMEM((2, top, rows), jnp.int32),
            pltpu.VMEM((units, 2, size, width), jnp.float32),
            pltpu.VMEM((units, width, 2 * size), jnp.bfloat16),
            pltpu.VMEM((units, width, 2 * size), jnp.bfloat16),
            pltpu.VMEM((2 * rows, width), jnp.float32),
            pltpu.VMEM((4 * rows, width), jnp.bfloat16),
            pltpu.VMEM((2 * rows, width), jnp.float32),
            pltpu.VMEM((top, 2 * rows, size), jnp.float32),
            pltpu.VMEM((top, 2 * rows, size), jnp.float32),
            pltpu.VMEM((top, 2 * rows, size), jnp.float32),
            pltpu.VMEM((2, rows, width), jnp.float32),
            pltpu.VMEM((2, 2, 8, rows), jnp.float32),
            pltpu.VMEM((rows, top, size), jnp.float32),
            dma((5,)),
            dma((12,)), dma((12,)),
            dma((12,)), dma((12,)),
            dma((10,)), dma((10,)),
            dma((22,)), dma((22,)),
            dma((7,)), dma((7,)),
        ],
        compiler_params=pltpu.CompilerParams(
            collective_id=0, has_side_effects=True, vmem_limit_bytes=VMEM_BYTES
        ),
    )(*[pltpu.with_memory_space_constraint(x, pltpu.HBM) for x in operands])


def solution(mesh):
    return jax.shard_map(
        device_program,
        mesh=mesh,
        in_specs=(
            P(("parts", "cluster"), None),
            P(("parts", "cluster"), None, None),
            P(("parts", "cluster"), None),
            P(("parts", "cluster"), None),
        ),
        out_specs=(P(("parts", "cluster"), None), P(("parts", "cluster"), None, None)),
        check_vma=False,
    )
```

time: 90.2 us -> 84.7 us (0.939)
  Pallas kernels: 87.9 us -> 82.3 us
    pallas_call x1, Pallas kernels: 87.9 us -> 82.3 us  [device_program(): pl.pallas_call(hub_kernel, out_shape=(jax.ShapeDtypeStruct((rows, width),...]
where the time goes in v3:
time: 84.7 us; the launch traced here: 84.4 us
  Pallas kernels  82.3 us (97%)
  local copies, waits for them, and re-layouts  1.5 us (2%)
    pallas_call x1, Pallas kernels, device_program(): pl.pallas_call(hub_kernel, out_shape=(jax.ShapeDtypeStruct((rows, width),...  82.3 us

profile of v3, /device:TPU:1, one launch (start us, length us, event | category | flops | bytes accessed | tf_op | source)
XLA Modules:
  0.0 84.4 jit_solution(7530645679004472838)
XLA Ops:
  0.6 82.3 %shard_map.59 = (f32[128,1024]{1,0:T(8,128)S(1)}, f32[128,4,128]{2,1,0:T(4,128)S(1)}) custom-call(f32[128,1024]{1,0:T(8,128)} %queries_in.1, f32[2,128,1024]{2,1,0:T(8,128)} %passages.1, s32[4,128]{1,0:T(4,128)} %bitcast.2, s32[4,128]{1,0:T(4,128)} %bitcast.3), custom_call_target="tpu_custom_call" | custom-call | tf_op jit(solution)/shard_map/pallas_call | solution.py:614
  82.9 0.8 copy.8
  83.7 0.7 copy.9

commit v4 on v3

--- a/solution.py
+++ b/solution.py
@@ -99,7 +99,9 @@
     return high, (x - high.astype(jnp.float32)).astype(jnp.bfloat16)
 
 
-def tools_of(corpus, turned_hi, turned_lo, pair, total, asked, names_of, part):
+def tools_of(
+    corpus, turned_hi, turned_lo, pair, total, asked, chosen, picked, names_of, part
+):
     both_rows = total.shape[0]
     top, _, size = asked.shape
     piece = size // 2
@@ -121,12 +123,7 @@
         group = pl.ds(0, count)
         highs, lows, names = [], [], []
         for unit, h in pieces:
-            high, low = halves(
-                jnp.concatenate([corpus[unit, 0, part(h), :], corpus[unit, 1, part(h), :]], axis=0)
-            )
-            place = pl.ds(h * size, size)
-            turned_hi[unit, :, place] = high.T
-            turned_lo[unit, :, place] = low.T
+            high, low = turn_over(unit, unit, h)
             highs.append(high)
             lows.append(low)
             own, others = names_of(unit)
@@ -161,7 +158,40 @@
         total[group, :] = total[group, :] * shrink + mixed
         return top_score, norm
 
-    return put_pair, spread_out, absorb
+    def turn_over(source, unit, h):
+        high, low = halves(
+            jnp.concatenate([corpus[source, 0, part(h), :], corpus[source, 1, part(h), :]], axis=0)
+        )
+        place = pl.ds(h * size, size)
+        turned_hi[unit, :, place] = high.T
+        turned_lo[unit, :, place] = low.T
+        return high, low
+
+    def score_units(g, rows, turns, starts, strides):
+        group = pl.ds(g * rows, rows)
+
+        def second_round(turn, carry):
+            values = [picked[j, group, :] for j in range(top)]
+            for start, stride in zip(starts, strides):
+                unit = start + stride * turn
+                found = dot_three(
+                    pair[group, :], pair[pl.ds(both_rows + g * rows, rows), :],
+                    turned_hi[unit], turned_lo[unit],
+                )
+                a, b = found[:, :size], found[:, size:]
+                own = jnp.where(lane < piece, a, pltpu.roll(b, piece, 1))
+                others = jnp.where(lane < piece, pltpu.roll(a, piece, 1), b)
+                names = names_of(unit)
+                for j in range(top):
+                    value = jnp.where(chosen[j, group, :] == names[0], own, values[j])
+                    values[j] = jnp.where(chosen[j, group, :] == names[1], others, value)
+            for j in range(top):
+                picked[j, group, :] = values[j]
+            return carry
+
+        lax.fori_loop(0, turns, second_round, 0)
+
+    return put_pair, spread_out, absorb, turn_over, score_units
 
 
 def dot_three(high, low, right_high, right_low):
@@ -312,12 +342,17 @@
         for unit in (2, 3):
             for h in range(2):
                 up(unit, h).start()
-        put_pair, spread_out, absorb = tools_of(
-            corpus, turned_hi, turned_lo, pair, total, asked, names_of, part
+        put_pair, spread_out, absorb, turn_over, score_units = tools_of(
+            corpus, turned_hi, turned_lo, pair, total, asked, chosen, picked, names_of, part
         )
         put_pair(queries[pl.ds(0, rows), :])
         spread_out(first, asked, 0)
+        spread_out(followup, chosen, 0)
         own = pl.ds(0, rows)
+        for k in range(2):
+            across(k).start()
+        for j in range(top):
+            picked[j, own, :] = jnp.zeros((rows, size), jnp.float32)
         total[own, :] = jnp.zeros((rows, width), jnp.float32)
         for copy, unit in zip(corner_side, (4, 5)):
             copy.wait_recv()
@@ -325,6 +360,11 @@
                 up(unit, h).start()
         for h in range(2):
             across_half(5, h).start()
+        across(4).start()
+        for source, unit in ((0, 2), (1, 3), (4, 4)):
+            across(source).wait_recv()
+            for h in range(2):
+                turn_over(source, unit, h)
         passed = [
             remote(
                 corpus.at[source, 0, part(h)], corpus.at[unit, 0, part(h)],
@@ -341,6 +381,8 @@
         for k in range(4):
             down(13 + k // 2, k % 2).wait_recv()
             passed[k].start()
+            if k % 2 == 1:
+                across(13 + k // 2).start()
             if k > 0:
                 share(k - 1)
         share(3)
@@ -351,6 +393,10 @@
             return absorb([(5, h), (10, h), (15, h)], rows, carry)
 
         peak, norm = lax.fori_loop(0, 2, late, nothing_yet(rows))
+        for unit in (13, 14):
+            across(unit).wait_recv()
+            for h in range(2):
+                turn_over(unit, unit, h)
         for k in range(2):
             back(k).wait_recv()
         early_peak, early_norm = (
@@ -360,8 +406,15 @@
         shrink, early_shrink = jnp.exp(peak - top_score), jnp.exp(early_peak - top_score)
         norm = norm * shrink + early_norm * early_shrink
         mixed = total[own, :] * shrink + early[1] * early_shrink
-        expanded[...] = queries[own, :] + (FEEDBACK * width ** (-0.5)) * (mixed / norm)
+        after = queries[own, :] + (FEEDBACK * width ** (-0.5)) * (mixed / norm)
+        expanded[...] = after
+        put_pair(after)
+        score_units(0, rows, 2, (2, 3, 4, 5), (8, 10, 10, 10))
         back(2).wait_recv()
+        for j in range(top):
+            scores[:, j, :] = scores[:, j, :] + picked[j, own, :]
+        for unit in (0, 1, 4, 13, 14):
+            across(unit).wait_send()
         for copy in passed:
             copy.wait_send()
         for unit in (5, 10, 15):
@@ -439,8 +492,8 @@
         ids_up(k).wait_recv()
     queries_up().wait_recv()
 
-    put_pair, spread_out, absorb = tools_of(
-        corpus, turned_hi, turned_lo, pair, total, asked, names_of, part
+    put_pair, spread_out, absorb, turn_over, score_units = tools_of(
+        corpus, turned_hi, turned_lo, pair, total, asked, chosen, picked, names_of, part
     )
     put_pair(queries[...])
     total[...] = jnp.zeros_like(total)
@@ -524,35 +577,13 @@
     put_pair(after)
     expanded[...] = after[:rows]
 
-    def score_all(g, out):
-        group = pl.ds(g * rows, rows)
-
-        def second_round(turn, carry):
-            values = [picked[j, group, :] for j in range(top)]
-            for k in range(4):
-                unit = 4 * turn + k
-                found = dot_three(
-                    pair[group, :], pair[pl.ds(both_rows + g * rows, rows), :],
-                    turned_hi[unit], turned_lo[unit],
-                )
-                a, b = found[:, :size], found[:, size:]
-                own = jnp.where(lane < piece, a, pltpu.roll(b, piece, 1))
-                others = jnp.where(lane < piece, pltpu.roll(a, piece, 1), b)
-                names = names_of(unit)
-                for j in range(top):
-                    value = jnp.where(chosen[j, group, :] == names[0], own, values[j])
-                    values[j] = jnp.where(chosen[j, group, :] == names[1], others, value)
-            for j in range(top):
-                picked[j, group, :] = values[j]
-            return carry
-
-        lax.fori_loop(0, 4, second_round, 0)
-        for j in range(top):
-            out[:, j, :] = picked[j, group, :]
-
-    score_all(1, scores_out)
+    score_units(1, rows, 2, (0, 1, 6, 7), (8, 8, 5, 5))
+    for j in range(top):
+        scores_out[:, j, :] = picked[j, pl.ds(rows, rows), :]
     back(2).start()
-    score_all(0, scores)
+    score_units(0, rows, 4, (0, 1, 2, 3), (4, 4, 4, 4))
+    for j in range(top):
+        scores[:, j, :] = picked[j, pl.ds(0, rows), :]
 
     for k in range(2):
         own_far(k).wait_send()

time: 84.7 us -> 82.3 us (0.972)
  Pallas kernels: 82.3 us -> 80.1 us
    pallas_call x1, Pallas kernels: 82.3 us -> 80.1 us  [device_program(): pl.pallas_call(hub_kernel, out_shape=(jax.ShapeDtypeStruct((rows, width),...]
where the time goes in v4:
time: 82.3 us; the launch traced here: 82.2 us
  Pallas kernels  80.1 us (97%)
  local copies, waits for them, and re-layouts  1.5 us (2%)
    pallas_call x1, Pallas kernels, device_program(): pl.pallas_call(hub_kernel, out_shape=(jax.ShapeDtypeStruct((rows, width),...  80.1 us

profile of v4, /device:TPU:1, one launch (start us, length us, event | category | flops | bytes accessed | tf_op | source)
XLA Modules:
  0.0 82.2 jit_solution(14818599893764531201)
XLA Ops:
  0.6 80.1 %shard_map.59 = (f32[128,1024]{1,0:T(8,128)S(1)}, f32[128,4,128]{2,1,0:T(4,128)S(1)}) custom-call(f32[128,1024]{1,0:T(8,128)} %queries_in.1, f32[2,128,1024]{2,1,0:T(8,128)} %passages.1, s32[4,128]{1,0:T(4,128)} %bitcast.2, s32[4,128]{1,0:T(4,128)} %bitcast.3), custom_call_target="tpu_custom_call" | custom-call | tf_op jit(solution)/shard_map/pallas_call | solution.py:645
  80.7 0.8 copy.8
  81.5 0.7 copy.9

commit v5 on v4

--- a/solution.py
+++ b/solution.py
@@ -107,10 +107,10 @@
     piece = size // 2
     lane = lax.broadcasted_iota(jnp.int32, (1, size), 1)
 
-    def put_pair(x):
+    def put_pair(x, offset=0):
         high, low = halves(x)
-        pair[pl.ds(0, x.shape[0]), :] = high
-        pair[pl.ds(both_rows, x.shape[0]), :] = low
+        pair[pl.ds(offset, x.shape[0]), :] = high
+        pair[pl.ds(both_rows + offset, x.shape[0]), :] = low
 
     def spread_out(held, wide, g):
         rows = held.shape[2]
@@ -118,9 +118,9 @@
             line = held[g, j : j + 1, :].astype(jnp.float32)
             wide[j, pl.ds(g * rows, rows), :] = jnp.broadcast_to(line, (size, rows)).T
 
-    def absorb(pieces, count, carry):
+    def absorb(pieces, count, carry, offset=0):
         peak, norm = carry
-        group = pl.ds(0, count)
+        group = pl.ds(offset, count)
         highs, lows, names = [], [], []
         for unit, h in pieces:
             high, low = turn_over(unit, unit, h)
@@ -133,7 +133,7 @@
             for turned in (turned_hi, turned_lo)
         ]
         all_found = dot_three(
-            pair[group, :], pair[pl.ds(both_rows, count), :], *wide
+            pair[group, :], pair[pl.ds(both_rows + offset, count), :], *wide
         )
         sums = [all_found[:, k * size : (k + 1) * size] for k in range(len(pieces))]
         parts, hits = [], []
@@ -361,10 +361,12 @@
         for h in range(2):
             across_half(5, h).start()
         across(4).start()
-        for source, unit in ((0, 2), (1, 3), (4, 4)):
+        for source, unit in ((0, 2), (1, 3)):
             across(source).wait_recv()
             for h in range(2):
                 turn_over(source, unit, h)
+        across(4).wait_recv()
+        carry = absorb([(4, 0), (4, 1)], rows, nothing_yet(rows))
         passed = [
             remote(
                 corpus.at[source, 0, part(h)], corpus.at[unit, 0, part(h)],
@@ -385,6 +387,8 @@
                 across(13 + k // 2).start()
             if k > 0:
                 share(k - 1)
+            if k == 2:
+                across(13).wait_recv()
         share(3)
 
         def late(h, carry):
@@ -392,11 +396,11 @@
                 across_half(unit, h).wait_recv()
             return absorb([(5, h), (10, h), (15, h)], rows, carry)
 
-        peak, norm = lax.fori_loop(0, 2, late, nothing_yet(rows))
-        for unit in (13, 14):
-            across(unit).wait_recv()
-            for h in range(2):
-                turn_over(unit, unit, h)
+        for h in range(2):
+            turn_over(13, 13, h)
+        across(14).wait_recv()
+        carry = absorb([(14, 0), (14, 1)], rows, carry)
+        peak, norm = lax.fori_loop(0, 2, late, carry)
         for k in range(2):
             back(k).wait_recv()
         early_peak, early_norm = (
@@ -508,6 +512,16 @@
 
     def step(t, carry):
         carry = take(4 + t, carry)
+
+        @pl.when(t == 5)
+        def _():
+            early[0] = total[pl.ds(rows, rows), :]
+            for k in range(2):
+                line = jnp.broadcast_to(carry[k][rows:], (rows, size)).T
+                stats[0, k] = line[: stats.shape[2], :]
+            back(1).start()
+            back(0).start()
+
         carry = take(t - 1, carry)
 
         @pl.when(t < 5)
@@ -553,14 +567,7 @@
     carry = take(0, carry)
     carry = lax.fori_loop(2, 6, step, carry)
 
-    early[0] = total[pl.ds(rows, rows), :]
-    for k in range(2):
-        line = jnp.broadcast_to(carry[k][rows:], (rows, size)).T
-        stats[0, k] = line[: stats.shape[2], :]
-    back(1).start()
-    back(0).start()
-
-    def finish(h, carry):
+    def arrive(h):
         from_mate(5, h).wait_recv()
         across_half(5, h).start()
         last_side(h).wait_recv()
@@ -569,18 +576,25 @@
         across_half(15, h).start()
         for unit in (5, 10, 15):
             across_half(unit, h).wait_recv()
-        return absorb([(5, h), (10, h), (15, h)], both_rows, carry)
-
-    _, norm = lax.fori_loop(0, 2, finish, carry)
-
-    after = queries[...] + (FEEDBACK * width ** (-0.5)) * (total[...] / norm)
-    put_pair(after)
-    expanded[...] = after[:rows]
-
+        return [(5, h), (10, h), (15, h)]
+
+    def expand(offset, norm):
+        group = pl.ds(offset, rows)
+        return queries[group, :] + (FEEDBACK * width ** (-0.5)) * (total[group, :] / norm)
+
+    carry = absorb(arrive(0), both_rows, carry)
+    _, norm = absorb(arrive(1), rows, (carry[0][rows:], carry[1][rows:]), rows)
+    put_pair(expand(rows, norm), rows)
     score_units(1, rows, 2, (0, 1, 6, 7), (8, 8, 5, 5))
     for j in range(top):
         scores_out[:, j, :] = picked[j, pl.ds(rows, rows), :]
     back(2).start()
+    _, norm = absorb(
+        [(unit, 1) for unit in (5, 10, 15)], rows, (carry[0][:rows], carry[1][:rows])
+    )
+    after = expand(0, norm)
+    put_pair(after)
+    expanded[...] = after
     score_units(0, rows, 4, (0, 1, 2, 3), (4, 4, 4, 4))
     for j in range(top):
         scores[:, j, :] = picked[j, pl.ds(0, rows), :]

time: 82.3 us -> 81.8 us (level)
  Pallas kernels: 80.1 us -> 79.2 us
    pallas_call x1, Pallas kernels: 80.1 us -> 79.2 us  [device_program(): pl.pallas_call(hub_kernel, out_shape=(jax.ShapeDtypeStruct((rows, width),...]
where the time goes in v5:
time: 81.8 us; the launch traced here: 81.3 us
  Pallas kernels  79.2 us (97%)
  local copies, waits for them, and re-layouts  1.5 us (2%)
    pallas_call x1, Pallas kernels, device_program(): pl.pallas_call(hub_kernel, out_shape=(jax.ShapeDtypeStruct((rows, width),...  79.2 us

profile of v5, /device:TPU:1, one launch (start us, length us, event | category | flops | bytes accessed | tf_op | source)
XLA Modules:
  0.0 81.3 jit_solution(17018889796055363439)
XLA Ops:
  0.6 79.2 %shard_map.59 = (f32[128,1024]{1,0:T(8,128)S(1)}, f32[128,4,128]{2,1,0:T(4,128)S(1)}) custom-call(f32[128,1024]{1,0:T(8,128)} %queries_in.1, f32[2,128,1024]{2,1,0:T(8,128)} %passages.1, s32[4,128]{1,0:T(4,128)} %bitcast.2, s32[4,128]{1,0:T(4,128)} %bitcast.3), custom_call_target="tpu_custom_call" | custom-call | tf_op jit(solution)/shard_map/pallas_call | solution.py:659
  79.8 0.8 copy.8
  80.6 0.7 copy.9
